TPU v7x, 1024 devices: a whole 8x8x8 slice. The times are simulated.
1024 devices in a mesh: dp: 8 (over y), expert: 8 (over x), group: 16 (over z, core).
Axes of the slice: x: 8, y: 8, z: 8, core: 2. Of those that a mesh axis runs over, the one named last changes fastest.
Arguments:
- tokens: bfloat16 [2048, 7168], P(('dp', 'group')), may hold values from -6 to 6
- expert_ids: int32 [2048, 8], P(('dp', 'group')), may hold values from 0 to 255, all different within a row; in each aligned block of 16 rows (0 to 15, 16 to 31, ...) at most 2 rows name the same one
- gate_values: bfloat16 [2048, 8], P(('dp', 'group')), may hold values from 0.099609375 to 1
- gate_up: bfloat16 [8, 7168, 2, 2048], P('expert', None, None, 'group'), may hold values from -0.0625 to 0.0625
- down_weight: bfloat16 [8, 2048, 7168], P('expert', 'group'), may hold values from -0.125 to 0.125
- shared_gate_up: bfloat16 [7168, 2, 2048], P('expert', None, 'group'), may hold values from -0.0625 to 0.0625
- shared_down: bfloat16 [2048, 7168], P('group', 'expert'), may hold values from -0.125 to 0.125
Outputs:
- mixed: bfloat16 [2048, 7168], P(('dp', 'group'), 'expert')
Inputs may be any that keep to these rules, and one draw needn't show every extreme that they name: `expert_ids`: each row names 8 different routed experts. In each aligned block of 16 rows (the rows of one device) no expert is named by more than 2 rows, and in some blocks one is named by exactly 2 rows.
All inputs are finite; a program needn't handle non-finite values.
Results may differ from a plain program's by a relative error of at most 0.028.
Values may be sent and summed in bfloat16 or wider, within the bound.
A program may use at most 64 MiB of HBM per device.

v0:
```python
import math

import jax
import jax.numpy as jnp
from jax import lax
from jax.sharding import PartitionSpec as P

CAP = 2


def sent_to_all(value, axis):
    copies = jnp.broadcast_to(value, (lax.axis_size(axis), *value.shape))
    return lax.all_to_all(copies, axis, split_axis=0, concat_axis=0, tiled=True)


def of_everyone(value, axis):
    return sent_to_all(value, axis).astype(jnp.float32).sum(axis=0)


def sent_together(arrays, axis, dim, along):
    widths = [math.prod(a.shape[along:]) for a in arrays]
    both = jnp.concatenate(
        [a.reshape(*a.shape[:along], w) for a, w in zip(arrays, widths)], axis=along
    )
    out = lax.all_gather(both, axis, axis=dim, tiled=True)
    blocks = jnp.split(out, [sum(widths[:k]) for k in range(1, len(widths))], axis=along)
    return tuple((b.reshape(*out.shape[:along], *a.shape[along:]) for a, b in zip(arrays, blocks)))


def split_up(value, dim, peers):
    before, after = (value.shape[:dim], value.shape[dim + 1 :])
    return jnp.moveaxis(value.reshape(*before, peers, -1, *after), dim, 0)


def sum_at_owner(value, axis, dim):
    peers = lax.axis_size(axis)
    blocks = lax.all_to_all(split_up(value, dim, peers), axis, 0, 0, tiled=True)
    return jnp.sum(blocks.astype(jnp.float32), axis=0)


def expert_terms(block_tokens, block_weight, gate_up, down_weight):
    model_width = gate_up.shape[1]
    hidden_units = gate_up.shape[3]
    projected = jnp.dot(
        block_tokens,
        gate_up[0].reshape(model_width, 2 * hidden_units),
        preferred_element_type=jnp.float32,
    )
    gate_part = projected[:, :hidden_units]
    up_part = projected[:, hidden_units:]
    hidden = (jax.nn.silu(gate_part) * up_part).astype(jnp.bfloat16)
    product = jnp.dot(hidden, down_weight[0], preferred_element_type=jnp.float32)
    return (product * block_weight.astype(jnp.float32)[:, None]).astype(jnp.bfloat16)


def shared_block(token_columns, shared_gate_up, shared_down):
    column_width = shared_gate_up.shape[0]
    shared_units = shared_gate_up.shape[2]
    shared_partial = jnp.dot(
        token_columns,
        shared_gate_up.reshape(column_width, 2 * shared_units),
        preferred_element_type=jnp.float32,
    )
    shared_pre = of_everyone(shared_partial.astype(jnp.bfloat16), "expert").astype(jnp.float32)
    shared_hidden = (
        jax.nn.silu(shared_pre[:, :shared_units]) * shared_pre[:, shared_units:]
    ).astype(jnp.bfloat16)
    return jnp.dot(shared_hidden, shared_down, preferred_element_type=jnp.float32).astype(
        jnp.bfloat16
    )


def per_device(tokens, expert_ids, gate_values, gate_up, down_weight, shared_gate_up, shared_down):
    slot_index = lax.axis_index("expert")
    column_width = shared_gate_up.shape[0]
    chosen = expert_ids == slot_index
    weight_value = jnp.sum(
        jnp.where(chosen, gate_values.astype(jnp.float32), jnp.float32(0.0)), axis=1
    )
    expert_count = lax.axis_size("expert")
    numbers = jnp.arange(expert_count, dtype=jnp.int32)
    named = jnp.any(expert_ids[None, :, :] == numbers[:, None, None], axis=2)
    position = jnp.cumsum(named.astype(jnp.int32), axis=1) - 1
    slot_numbers = jnp.arange(CAP, dtype=jnp.int32)
    pickers = ((position[:, None, :] == slot_numbers[None, :, None]) & named[:, None, :]).astype(
        jnp.float32
    )
    own_picker = lax.dynamic_index_in_dim(pickers, slot_index, 0, keepdims=False)
    packed = jnp.dot(
        own_picker.astype(jnp.bfloat16), tokens, preferred_element_type=jnp.float32
    ).astype(jnp.bfloat16)
    packed_weight = jnp.dot(own_picker, weight_value).astype(jnp.bfloat16)
    own_columns = lax.dynamic_slice_in_dim(tokens, slot_index * column_width, column_width, 1)
    all_rows, all_weight, all_columns = (
        *sent_together((packed, packed_weight), "group", 0, 1),
        lax.all_gather(own_columns, "group", axis=0, tiled=True),
    )
    shared_term = shared_block(all_columns, shared_gate_up, shared_down)
    routed = expert_terms(all_rows, all_weight, gate_up, down_weight)
    own_rows, shared_rows = (
        sum_at_owner(routed.astype(jnp.float32).astype(jnp.bfloat16), "group", 0),
        sum_at_owner(shared_term.astype(jnp.float32).astype(jnp.bfloat16), "group", 0),
    )
    received = lax.all_to_all(
        own_rows.astype(jnp.bfloat16), "expert", split_axis=1, concat_axis=0, tiled=True
    ).astype(own_rows.dtype)
    placed = jnp.einsum("ect,ecd->td", pickers, received.reshape(expert_count, CAP, column_width))
    mixed = placed + shared_rows
    return mixed.astype(jnp.bfloat16)


def solution(mesh):
    in_specs = (
        P(("dp", "group"), None),
        P(("dp", "group"), None),
        P(("dp", "group"), None),
        P("expert", None, None, "group"),
        P("expert", "group", None),
        P("expert", None, "group"),
        P("group", "expert"),
    )
    out_specs = P(("dp", "group"), "expert")
    return jax.shard_map(
        per_device, mesh=mesh, in_specs=in_specs, out_specs=out_specs, check_vma=False
    )
```

profile of v0, /device:TPU:1, one launch (start us, length us, event | category | flops | bytes accessed | tf_op | source)
XLA Modules:
  0.0 120.5 jit_solution(7767140626327193369)
XLA Ops:
  0.0 0.9 constant_dynamic-slice_fusion
  0.9 32.1 %all_gather.7 = bf16[256,896]{1,0:T(8,128)(2,1)S(1)} all-gather(bf16[16,896]{1,0:T(8,128)(2,1)S(1)} %constant_dynamic-slice_fusion), channel_id=1, replica_groups=mesh['dp'=8,'expert'=8,'group'=16] {'group'}, dimensions={0}, use_global_device_ids=true | all-gather | bytes 487424 | tf_op jit(solution)/shard_map/all_gather | solution.py:96
  33.0 1.3 %convolution_convert_fusion.2 = bf16[256,256]{1,0:T(8,128)(2,1)S(1)} fusion(bf16[256,896]{1,0:T(8,128)(2,1)S(1)} %all_gather.7, bf16[112,8,2,128]{3,2,1,0:T(2,128)(2,1)} %bitcast.49), kind=kOutput, calls=%fused_computation.9 | convolution fusion | flops 117506048 | bytes 1048576 | tf_op jit(solution)/shard_map/dot_general | solution.py:59
  34.3 1.1 broadcast_in_dim.7
  35.4 6.5 %all-to-all-start.2 = ((bf16[8,256,256]{2,1,0:T(8,128)(2,1)}), bf16[8,256,256]{2,1,0:T(8,128)(2,1)S(1)}, u32[]{:S(2)}, u32[]{:S(2)}) async-start(bf16[8,256,256]{2,1,0:T(8,128)(2,1)} %broadcast_in_dim.7), calls=%async_computation.2 | async-start | bytes 2097152 | tf_op jit(solution)/shard_map/all_to_all | solution.py:13
  41.9 0.0 copy-done.2
  41.9 0.0 copy-done.3
  42.0 0.2 reduce_window_sum.11
  42.1 0.0 copy-done.1
  42.2 0.2 convolution_convert_fusion
  42.3 0.1 fusion.8
  42.4 0.1 copy.17
  42.6 15.8 %all-gather = bf16[16,2,7169]{2,1,0:T(2,128)(2,1)S(1)} all-gather(bf16[1,2,7169]{2,1,0:T(2,128)(2,1)S(1)} %maximum_bitcast_fusion), channel_id=1, replica_groups=mesh['dp'=8,'expert'=8,'group'=16] {'group'}, dimensions={0}, use_global_device_ids=true | all-gather | bytes 487492 | tf_op jit(solution)/shard_map/all_gather | solution.py:25
  58.4 1.1 reshape.36
  59.6 0.7 split.9
  60.2 0.1 copy.21
  60.4 2.9 %fusion.1 = f32[32,256]{1,0:T(8,128)S(1)} fusion(bf16[896,8,2,128]{3,2,1,0:T(2,128)(2,1)} %bitcast.48, bf16[32,7169]{1,0:T(8,128)(2,1)} %reshape.36), kind=kOutput, calls=%fused_computation.3 | convolution fusion | flops 117440512 | bytes 4161536 | tf_op jit(solution)/shard_map/dot_general | solution.py:44
  63.3 0.0 copy-done
  63.3 0.4 fusion
  63.7 1.0 reshape.31
  64.6 6.5 %all-to-all-done.2 = bf16[8,256,256]{2,1,0:T(8,128)(2,1)S(1)} async-done(((bf16[8,256,256]{2,1,0:T(8,128)(2,1)}), bf16[8,256,256]{2,1,0:T(8,128)(2,1)S(1)}, u32[]{:S(2)}, u32[]{:S(2)}) %all-to-all-start.2) | async-done | bytes 1048608 | tf_op jit(solution)/shard_map/all_to_all | solution.py:13
  71.1 3.8 %all-to-all-start = ((bf16[16,2,7168]{2,1,0:T(2,128)(2,1)}), bf16[16,2,7168]{2,1,0:T(2,128)(2,1)S(1)}, u32[]{:S(2)}, u32[]{:S(2)}) async-start(bf16[16,2,7168]{2,1,0:T(2,128)(2,1)} %reshape.31), calls=%async_computation | async-start | bytes 917504 | tf_op jit(solution)/shard_map/all_to_all | solution.py:37
  75.0 0.1 convert_reduce_fusion
  75.1 2.0 %convolution_convert_fusion.1 = bf16[256,896]{1,0:T(8,128)(2,1)} fusion(bf16[128,896]{1,0:T(8,128)(2,1)} %param.13, f32[256,256]{1,0:T(8,128)S(1)} %convert_reduce_fusion), kind=kOutput, calls=%fused_computation.8 | convolution fusion | flops 59146240 | bytes 950272 | tf_op jit(solution)/shard_map/dot_general | solution.py:68
  77.1 13.8 %all-to-all-done = bf16[16,2,7168]{2,1,0:T(2,128)(2,1)S(1)} async-done(((bf16[16,2,7168]{2,1,0:T(2,128)(2,1)}), bf16[16,2,7168]{2,1,0:T(2,128)(2,1)S(1)}, u32[]{:S(2)}, u32[]{:S(2)}) %all-to-all-start) | async-done | bytes 458784 | tf_op jit(solution)/shard_map/all_to_all | solution.py:37
  90.9 3.5 %all-to-all-start.3 = ((bf16[16,16,896]{2,1,0:T(8,128)(2,1)}), bf16[16,16,896]{2,1,0:T(8,128)(2,1)S(1)}, u32[]{:S(2)}, u32[]{:S(2)}) async-start(bf16[16,16,896]{2,1,0:T(8,128)(2,1)} %bitcast.11), calls=%async_computation.3 | async-start | bytes 917504 | tf_op jit(solution)/shard_map/all_to_all | solution.py:37
  94.4 1.0 reduce_sum.40
  95.4 14.3 %all-to-all-done.3 = bf16[16,16,896]{2,1,0:T(8,128)(2,1)S(1)} async-done(((bf16[16,16,896]{2,1,0:T(8,128)(2,1)}), bf16[16,16,896]{2,1,0:T(8,128)(2,1)S(1)}, u32[]{:S(2)}, u32[]{:S(2)}) %all-to-all-start.3) | async-done | bytes 458784 | tf_op jit(solution)/shard_map/all_to_all | solution.py:37
  109.6 3.3 %all-to-all-start.1 = ((bf16[2,8,896]{2,0,1:T(2,128)(2,1)}), bf16[2,8,896]{2,0,1:T(2,128)(2,1)S(1)}, u32[]{:S(2)}, u32[]{:S(2)}) async-start(bf16[2,8,896]{2,0,1:T(2,128)(2,1)} %bitcast.8), calls=%async_computation.1 | async-start | bytes 57344 | tf_op jit(solution)/shard_map/all_to_all | solution.py:104
  113.0 0.1 convert_reduce_fusion.1
  113.1 6.7 %all-to-all-done.1 = bf16[2,8,896]{2,0,1:T(2,128)(2,1)S(1)} async-done(((bf16[2,8,896]{2,0,1:T(2,128)(2,1)}), bf16[2,8,896]{2,0,1:T(2,128)(2,1)S(1)}, u32[]{:S(2)}, u32[]{:S(2)}) %all-to-all-start.1) | async-done | bytes 28704 | tf_op jit(solution)/shard_map/all_to_all | solution.py:104
  119.7 0.8 fusion.6
  (11 shorter events, 0.1 us)
Async XLA Ops:
  0.0 63.3 %copy-start = (bf16[1,128,7168]{2,1,0:T(8,128)(2,1)S(1)}, bf16[1,128,7168]{2,1,0:T(8,128)(2,1)}, u32[]{:S(2)}) copy-start(bf16[1,128,7168]{2,1,0:T(8,128)(2,1)} %param.11) | copy-start | bytes 5505028
  0.0 42.1 %copy-start.1 = (bf16[16,7168]{1,0:T(8,128)(2,1)S(1)}, bf16[16,7168]{1,0:T(8,128)(2,1)}, u32[]{:S(2)}) copy-start(bf16[16,7168]{1,0:T(8,128)(2,1)} %param.7) | copy-start | bytes 688132
  0.0 41.9 %copy-start.2 = (s32[16,8]{0,1:T(8,128)S(1)}, s32[16,8]{0,1:T(8,128)}, u32[]{:S(2)}) copy-start(s32[16,8]{0,1:T(8,128)} %param.8) | copy-start | bytes 1540
  0.0 41.9 %copy-start.3 = (bf16[16,8]{0,1:T(8,128)(2,1)S(1)}, bf16[16,8]{0,1:T(8,128)(2,1)}, u32[]{:S(2)}) copy-start(bf16[16,8]{0,1:T(8,128)(2,1)} %param.9) | copy-start | bytes 772
  35.4 35.7 %all-to-all-start.2 = ((bf16[8,256,256]{2,1,0:T(8,128)(2,1)}), bf16[8,256,256]{2,1,0:T(8,128)(2,1)S(1)}, u32[]{:S(2)}, u32[]{:S(2)}) async-start(bf16[8,256,256]{2,1,0:T(8,128)(2,1)} %broadcast_in_dim.7), calls=%async_computation.2 | async-start | bytes 2097152 | tf_op jit(solution)/shard_map/all_to_all | solution.py:13
  71.1 19.8 %all-to-all-start = ((bf16[16,2,7168]{2,1,0:T(2,128)(2,1)}), bf16[16,2,7168]{2,1,0:T(2,128)(2,1)S(1)}, u32[]{:S(2)}, u32[]{:S(2)}) async-start(bf16[16,2,7168]{2,1,0:T(2,128)(2,1)} %reshape.31), calls=%async_computation | async-start | bytes 917504 | tf_op jit(solution)/shard_map/all_to_all | solution.py:37
  90.9 18.7 %all-to-all-start.3 = ((bf16[16,16,896]{2,1,0:T(8,128)(2,1)}), bf16[16,16,896]{2,1,0:T(8,128)(2,1)S(1)}, u32[]{:S(2)}, u32[]{:S(2)}) async-start(bf16[16,16,896]{2,1,0:T(8,128)(2,1)} %bitcast.11), calls=%async_computation.3 | async-start | bytes 917504 | tf_op jit(solution)/shard_map/all_to_all | solution.py:37
  109.6 10.1 %all-to-all-start.1 = ((bf16[2,8,896]{2,0,1:T(2,128)(2,1)}), bf16[2,8,896]{2,0,1:T(2,128)(2,1)S(1)}, u32[]{:S(2)}, u32[]{:S(2)}) async-start(bf16[2,8,896]{2,0,1:T(2,128)(2,1)} %bitcast.8), calls=%async_computation.1 | async-start | bytes 57344 | tf_op jit(solution)/shard_map/all_to_all | solution.py:104
where the time goes:
time: 121 us
  blocking collectives  47.9 us (40%)
  waiting for transfers between devices  41.2 us (34%)
  starting transfers between devices  17.1 us (14%)
  matrix products  7.7 us (6%)
  local copies, waits for them, and re-layouts  4.98 us (4%)
  other arithmetic  1.49 us (1%)
    all_gather x1, blocking collectives, per_device(): lax.all_gather(own_columns, 'group', axis=0, tiled=True)  32.1 us
    all_to_all x2, waiting for transfers between devices, sum_at_owner(): blocks = lax.all_to_all(split_up(value, dim, peers), axis, 0, 0, tiled=True)  28.1 us
    all_gather x1, blocking collectives, sent_together(): out = lax.all_gather(both, axis, axis=dim, tiled=True)  15.8 us
    all_to_all x2, starting transfers between devices, sum_at_owner(): blocks = lax.all_to_all(split_up(value, dim, peers), axis, 0, 0, tiled=True)  7.29 us
    all_to_all x1, waiting for transfers between devices, per_device(): lax.all_to_all(own_rows.astype(jnp.bfloat16), 'expert', split_axis=1, con...  6.68 us
    all_to_all x1, waiting for transfers between devices, sent_to_all(): return lax.all_to_all(copies, axis, split_axis=0, concat_axis=0, tiled=True)  6.49 us
    all_to_all x1, starting transfers between devices, sent_to_all(): return lax.all_to_all(copies, axis, split_axis=0, concat_axis=0, tiled=True)  6.48 us
    all_to_all x1, starting transfers between devices, per_device(): lax.all_to_all(own_rows.astype(jnp.bfloat16), 'expert', split_axis=1, con...  3.34 us
  transfers between devices with their start and end apart: 4, of which 4 were waited for; matrix products, arithmetic and copies ran while one was open for 8% of the time, Pallas kernels for 0%

commit v1 on v0

v1 whole, which is shorter than its diff:
```python
import functools

import jax
import jax.numpy as jnp
from jax import lax
from jax.experimental import pallas as pl
from jax.experimental.pallas import tpu as pltpu
from jax.sharding import PartitionSpec as P

MESH = pl.DeviceIdType.MESH
CAP = 2
F32, BF16 = jnp.float32, jnp.bfloat16
GATHER_S, GATHER_R, SPREAD, SHARE, RETURN_R, RETURN_S = range(6)
SENDS, ARRIVALS = 6, 3


def iota(shape, dim):
    return lax.broadcasted_iota(jnp.int32, shape, dim)


def one_hot(condition):
    return jnp.where(condition, 1.0, 0.0).astype(BF16)


def dot(a, b):
    return jnp.dot(a, b, preferred_element_type=F32)


def swap_matrix(n):
    rows = 2 * n * n
    to, source = iota((rows, rows), 0), iota((rows, rows), 1)
    major, minor, pick = to // (2 * n), to % (2 * n) // 2, to % 2
    return one_hot(source == minor * (2 * n) + major * 2 + pick)


def kernel(
    n,
    tok_hbm,
    ids_hbm,
    val_hbm,
    w1_hbm,
    w2_hbm,
    s1_hbm,
    s2_hbm,
    out_ref,
    tok,
    ids,
    val,
    w1,
    w2,
    s1,
    s2,
    s1d,
    xs,
    xr,
    part,
    parts,
    hid,
    hids,
    spread,
    y,
    placed,
    ret_s,
    got_s,
    swap,
    expand,
    apart,
    local_sem,
    pair_send,
    pair_recv,
    send_sem,
    recv_sem,
):
    x = lax.axis_index("expert")
    g = lax.axis_index("group")
    z, c = g // 2, g % 2
    rows, width = tok.shape[1], tok.shape[2]
    units = w2.shape[1]
    pieces = width // 128
    total = n * rows

    def z_peer(k):
        return {"group": (z + k) % n * 2 + c}

    def x_peer(k):
        return {"expert": (x + k) % n}

    sibling = {"group": z * 2 + 1 - c}

    columns = pltpu.make_async_copy(
        tok_hbm.at[:, pl.ds(pl.multiple_of(x * width, 128), width)], xs.at[z], local_sem.at[6]
    )
    columns.start()
    barrier = pltpu.get_barrier_semaphore()
    peers = [z_peer(k) for k in (2, n - 2, 1, n - 1)] + [sibling]
    peers += [x_peer(k) for k in range(1, n)]
    for peer in peers:
        pl.semaphore_signal(barrier, inc=1, device_id=peer, device_id_type=MESH)

    tokens = [
        pltpu.make_async_copy(
            tok_hbm.at[:, pl.ds(j * width, width)], tok.at[j], local_sem.at[7]
        )
        for j in range(n)
    ]
    loads = [
        pltpu.make_async_copy(source, target, local_sem.at[i])
        for i, (source, target) in enumerate(
            (
                (ids_hbm, ids),
                (val_hbm, val),
                (s1_hbm, s1.at[c]),
                (s2_hbm, s2.at[c]),
                (w1_hbm, w1.at[c]),
                (w2_hbm, w2.at[c]),
            )
        )
    ]
    for copy in [*tokens, *loads]:
        copy.start()

    def send(phase, step, source, target, peer):
        pltpu.make_async_remote_copy(
            src_ref=source,
            dst_ref=target,
            send_sem=send_sem.at[phase],
            recv_sem=recv_sem.at[phase, step],
            device_id=peer,
            device_id_type=MESH,
        ).start()

    def bytes_of(ref, sem):
        pltpu.make_async_copy(ref, ref, sem).wait()

    def arrived(phase, step, target):
        bytes_of(target, recv_sem.at[phase, step])

    upper = z >= n // 2
    middle = (z >= 2) & (z < n - 2)

    far_first = sorted(range(1, n), key=lambda k: (-min(k, n - k), k))
    def at(k):
        return (z + k + n) % n

    def gather_start(phase, block, steps):
        for k in steps:
            send(phase, {2: 0, -2: 1}.get(k, 2), block.at[z], block.at[z], z_peer(k % n))

    def relay(phase, block, sign):
        source = at(-2 * sign)
        arrived(phase, 0 if sign > 0 else 1, block.at[source])
        send(phase, 2, block.at[source], block.at[source], z_peer(sign % n))

        @pl.when(middle)
        def _():
            send(phase, 2, block.at[source], block.at[source], z_peer(2 * sign % n))

    def in_turn(*steps):
        @pl.when(upper)
        def _():
            for sign in (1, -1):
                for step in steps:
                    step(sign)

        @pl.when(jnp.logical_not(upper))
        def _():
            for sign in (-1, 1):
                for step in steps:
                    step(sign)

    def gather_end(phase, block):
        arrived(phase, 2, block.at[pl.ds(0, 5)])

    def gather_sent(phase, block):
        @pl.when(middle)
        def _():
            bytes_of(block, send_sem.at[phase])

        @pl.when(jnp.logical_not(middle))
        def _():
            bytes_of(block.at[pl.ds(0, 6)], send_sem.at[phase])

    columns.wait()
    pl.semaphore_wait(barrier, len(peers))
    gather_start(GATHER_S, xs, (2, -2, 1, -1))
    pairs = [
        pltpu.make_async_remote_copy(
            src_ref=source,
            dst_ref=target.at[c],
            send_sem=pair_send.at[i],
            recv_sem=pair_recv.at[i],
            device_id=sibling,
            device_id_type=MESH,
        )
        for i, (source, target) in enumerate(
            ((s1_hbm, s1), (w1_hbm, w1), (w2_hbm, w2), (s2_hbm, s2))
        )
    ]
    pairs[0].start()

    bytes_of(tok, local_sem.at[7])
    loads[0].wait()
    named = jnp.sum(jnp.where(ids[...] == x, 1.0, 0.0), axis=0, keepdims=True)
    named = jnp.broadcast_to(named, (8, rows)).astype(BF16)
    token, lane = iota((rows, total), 0), iota((rows, total), 1)
    named_at = dot(named, one_hot(lane % rows == token))[0:1]
    place_of = dot(named, one_hot(token < lane % rows))[0:1]
    row, lane = iota((CAP * n, total), 0), iota((CAP * n, total), 1)
    picker = (named_at > 0.5) & (place_of.astype(jnp.int32) == row % CAP)
    picker = one_hot(picker & (row // CAP == lane // rows))
    packed = dot(picker, tok[...].reshape(total, width)).astype(BF16)
    xr[z] = packed
    gather_start(GATHER_R, xr, (2, -2, 1, -1))
    for copy in pairs[1:]:
        copy.start()

    def pair_arrived(i, target):
        pltpu.make_async_remote_copy(
            src_ref=target.at[1 - c],
            dst_ref=target.at[1 - c],
            send_sem=pair_send.at[i],
            recv_sem=pair_recv.at[i],
            device_id=sibling,
            device_id_type=MESH,
        ).wait_recv()

    swap[...] = swap_matrix(n)
    feature, lane = iota((128, 512), 0), iota((128, 512), 1)
    expand[...] = one_hot(lane % 256 == feature * 2 + lane // 256)
    to, source = iota((256, 256), 0), iota((256, 256), 1)
    apart[...] = one_hot(source == to % 128 * 2 + to // 128)

    loads[1].wait()
    number = iota((CAP * n, rows), 0)
    holds = jnp.zeros((CAP * n, rows), F32)
    weight = jnp.zeros((CAP * n, rows), F32)
    for k in range(ids.shape[0]):
        same = ids[k : k + 1, :] == number // CAP
        holds = holds + jnp.where(same, 1.0, 0.0)
        weight = weight + jnp.where(same, val[k : k + 1, :].astype(F32), 0.0)
    before = one_hot(iota((rows, rows), 0) < iota((rows, rows), 1))
    place_all = dot(holds.astype(BF16), before).astype(jnp.int32)
    combine = jnp.where((holds > 0.5) & (place_all == number % CAP), weight, 0.0).astype(BF16)

    in_turn(
        functools.partial(relay, GATHER_S, xs),
        functools.partial(relay, GATHER_R, xr),
    )

    loads[2].wait()
    pair_arrived(0, s1)
    for q in range(pieces):
        both = jnp.concatenate([s1[i, q * 256 : q * 256 + 256, :] for i in range(2)], axis=1)
        split = dot(apart[...], both).astype(BF16)
        s1d[q * 128 : q * 128 + 128, 0 : 2 * units] = split[:128]
        s1d[q * 128 : q * 128 + 128, 2 * units : 4 * units] = split[128:]

    gather_end(GATHER_S, xs)
    mine = dot(xs[...].reshape(total, width), s1d[...]).astype(BF16)
    part[...] = mine.reshape(n, rows, 4 * units)
    for k in far_first:
        send(SPREAD, 0, part.at[(x + k) % n], parts.at[x], x_peer(k))
    parts[x] = part[x]

    gather_end(GATHER_R, xr)
    regrouped = dot(swap[...], xr[...].reshape(total, width)).astype(BF16)
    stacked = jnp.concatenate(
        [regrouped[:, q * 128 : q * 128 + 128] for q in range(pieces)], axis=0
    )
    spread[...] = dot(stacked, expand[...]).astype(BF16).reshape(pieces, n, CAP * n, 512)

    loads[4].wait()
    pair_arrived(1, w1)
    left = jnp.concatenate(
        [
            jnp.concatenate(
                [
                    spread[q, j, :, h * 256 : h * 256 + 256]
                    for j in range(n)
                    for q in range(pieces)
                ],
                axis=1,
            )
            for h in range(2)
        ],
        axis=0,
    )
    both = dot(left, jnp.concatenate([w1[0], w1[1]], axis=1))
    gate, up = both[: CAP * n], both[CAP * n :]
    routed = (gate / (1.0 + jnp.exp(-gate)) * up).astype(BF16)

    arrived(SPREAD, 0, parts.at[pl.ds(0, n - 1)])
    pre = jnp.sum(parts[...].astype(F32), axis=0)
    gate, up = pre[:, : 2 * units], pre[:, 2 * units :]
    hidden = (gate / (1.0 + jnp.exp(-gate)) * up).astype(BF16)
    hid[...] = hidden
    for k in far_first:
        send(SHARE, 0, hid, hids.at[x], x_peer(k))
    hids[x] = hidden

    loads[5].wait()
    pair_arrived(2, w2)
    here = z * n + x
    for m in range(n):
        j = (x + m) % n
        columns = w2[:, :, pl.ds(pl.multiple_of(j * width, 128), width)]
        y[m] = dot(routed, columns.reshape(2 * units, width)).astype(BF16).reshape(n, CAP, width)
        for k in [*far_first, 0] if m else far_first:
            peer = {"expert": j, "group": at(k) * 2 + c}
            send(RETURN_R, 0, y.at[m, at(k)], placed.at[here], peer)
    placed[here] = y[0, z]

    loads[3].wait()
    pair_arrived(3, s2)
    arrived(SHARE, 0, hids.at[pl.ds(0, n - 1)])
    shared = dot(hids[...].reshape(total, 2 * units), s2[...].reshape(2 * units, width))
    ret_s[...] = shared.astype(BF16).reshape(n, rows, width)
    for k in far_first:
        send(RETURN_S, 0, ret_s.at[at(k)], got_s.at[z], z_peer(k))
    got_s[z] = ret_s[z]

    arrived(RETURN_R, 0, placed.at[pl.ds(0, n * n - 1)])
    routed_rows = lax.dot_general(
        jnp.concatenate([combine] * n, axis=0),
        placed[...].reshape(CAP * n * n, width),
        (((0,), (0,)), ((), ())),
        preferred_element_type=F32,
    )
    arrived(RETURN_S, 0, got_s.at[pl.ds(0, n - 1)])
    shared_rows = jnp.sum(got_s[...].astype(F32), axis=0)
    out_ref[...] = (routed_rows + shared_rows).astype(BF16)

    gather_sent(GATHER_S, xs)
    gather_sent(GATHER_R, xr)
    bytes_of(parts.at[pl.ds(0, n - 1)], send_sem.at[SPREAD])
    bytes_of(hids.at[pl.ds(0, n - 1)], send_sem.at[SHARE])
    bytes_of(placed.at[pl.ds(0, n * n - 1)], send_sem.at[RETURN_R])
    bytes_of(got_s.at[pl.ds(0, n - 1)], send_sem.at[RETURN_S])
    for copy in pairs:
        copy.wait_send()


def solution(mesh):
    n = mesh.shape["expert"]

    def layer(tokens, expert_ids, gate_values, gate_up, down_weight, shared_gate_up, shared_down):
        rows, features = tokens.shape
        width = features // n
        units = gate_up.shape[3]
        top = expert_ids.shape[1]
        hbm = pl.BlockSpec(memory_space=pltpu.MemorySpace.HBM)
        vmem = pl.BlockSpec(memory_space=pltpu.VMEM)
        block = pltpu.VMEM((n, rows, width), BF16)
        packed = pltpu.VMEM((n, CAP * n, width), BF16)
        return pl.pallas_call(
            functools.partial(kernel, n),
            name="moe_layer",
            out_shape=pltpu.VMEM((rows, width), BF16),
            in_specs=[hbm] * 7,
            out_specs=vmem,
            scratch_shapes=[
                block,
                pltpu.VMEM((top, rows), jnp.int32),
                pltpu.VMEM((top, rows), BF16),
                pltpu.VMEM((2, 2 * features, units), BF16),
                pltpu.VMEM((2, units, features), BF16),
                pltpu.VMEM((2, 2 * width, units), BF16),
                pltpu.VMEM((2, units, width), BF16),
                pltpu.VMEM((width, 4 * units), BF16),
                block,
                packed,
                pltpu.VMEM((n, rows, 4 * units), BF16),
                pltpu.VMEM((n, rows, 4 * units), BF16),
                pltpu.VMEM((rows, 2 * units), BF16),
                pltpu.VMEM((n, rows, 2 * units), BF16),
                pltpu.VMEM((width // 128, n, CAP * n, 512), BF16),
                pltpu.VMEM((n, n, CAP, width), BF16),
                pltpu.VMEM((n * n, CAP, width), BF16),
                block,
                block,
                pltpu.VMEM((CAP * n * n, CAP * n * n), BF16),
                pltpu.VMEM((128, 512), BF16),
                pltpu.VMEM((256, 256), BF16),
                pltpu.SemaphoreType.DMA((8,)),
                pltpu.SemaphoreType.DMA((4,)),
                pltpu.SemaphoreType.DMA((4,)),
                pltpu.SemaphoreType.DMA((SENDS,)),
                pltpu.SemaphoreType.DMA((SENDS, ARRIVALS)),
            ],
            compiler_params=pltpu.CompilerParams(
                collective_id=0, has_side_effects=True, vmem_limit_bytes=48 << 20
            ),
        )(
            *(
                pltpu.with_memory_space_constraint(a, pltpu.MemorySpace.HBM)
                for a in (
                    tokens,
                    expert_ids.T,
                    gate_values.T,
                    gate_up.reshape(2 * features, units),
                    down_weight.reshape(units, features),
                    shared_gate_up.reshape(2 * width, units),
                    shared_down,
                )
            )
        )

    return jax.shard_map(
        layer,
        mesh=mesh,
        in_specs=(
            P(("dp", "group"), None),
            P(("dp", "group"), None),
            P(("dp", "group"), None),
            P("expert", None, None, "group"),
            P("expert", "group", None),
            P("expert", None, "group"),
            P("group", "expert"),
        ),
        out_specs=P(("dp", "group"), "expert"),
        check_vma=False,
    )
```

time: 121 us -> 47.7 us (0.39)
  the two profiles are of different devices: /device:TPU:1 before, /device:TPU:96 now
where the time goes in v1:
time: 47.7 us; the launch traced here: 47.5 us
  Pallas kernels  46.9 us (98%)
  local copies, waits for them, and re-layouts  0.61 us (1%)
    pallas_call x1, Pallas kernels, layer(): pl.pallas_call(functools.partial(kernel, n), name='moe_layer', out_shape=...  46.9 us

profile of v1, /device:TPU:96, one launch (start us, length us, event | category | flops | bytes accessed | tf_op | source)
XLA Modules:
  0.0 47.5 jit_solution(13692248572660557064)
XLA Ops:
  0.0 46.9 %moe_layer.1 = bf16[16,896]{1,0:T(8,128)(2,1)S(1)} custom-call(bf16[16,7168]{1,0:T(8,128)(2,1)} %tok_hbm.1, s32[8,16]{1,0:T(8,128)} %bitcast.8, bf16[8,16]{1,0:T(8,128)(2,1)} %bitcast.9, bf16[14336,128]{1,0:T(8,128)(2,1)} %bitcast.5, bf16[128,7168]{1,0:T(8,128)(2,1)} %bitcast.6, bf16[1792,128]{1,0:T(8,128)(2,1)} %bitcast.7, bf16[128,896]{1,0:T(8,128)(2,1)} %s2_hbm.1), custom_call_target="tpu_custom_call" | custom-call | tf_op jit(solution)/shard_map/moe_layer/pallas_call | solution.py:355
  46.9 0.6 %copy.9 = bf16[16,896]{1,0:T(8,128)(2,1)} copy(bf16[16,896]{1,0:T(8,128)(2,1)S(1)} %moe_layer.1) | data formatting | bytes 57344

commit v2 on v1

--- a/solution.py
+++ b/solution.py
@@ -70,6 +70,7 @@
     pair_recv,
     send_sem,
     recv_sem,
+    ready_sem,
 ):
     x = lax.axis_index("expert")
     g = lax.axis_index("group")
@@ -92,8 +93,15 @@
     )
     columns.start()
     barrier = pltpu.get_barrier_semaphore()
-    peers = [z_peer(k) for k in (2, n - 2, 1, n - 1)] + [sibling]
+    peers = [z_peer(n - 2), z_peer(n - 1), sibling]
     peers += [x_peer(k) for k in range(1, n)]
+
+    for k in (2, 1):
+
+        @pl.when(z < n - k)
+        def _():
+            pl.semaphore_signal(barrier, inc=1, device_id=z_peer(k), device_id_type=MESH)
+
     for peer in peers:
         pl.semaphore_signal(barrier, inc=1, device_id=peer, device_id_type=MESH)
 
@@ -135,7 +143,7 @@
     def arrived(phase, step, target):
         bytes_of(target, recv_sem.at[phase, step])
 
-    upper = z >= n // 2
+    upper = z >= 2
     middle = (z >= 2) & (z < n - 2)
 
     far_first = sorted(range(1, n), key=lambda k: (-min(k, n - k), k))
@@ -144,7 +152,34 @@
 
     def gather_start(phase, block, steps):
         for k in steps:
-            send(phase, {2: 0, -2: 1}.get(k, 2), block.at[z], block.at[z], z_peer(k % n))
+
+            @pl.when(z >= -k)
+            def _():
+                own_to(phase, block, k)
+
+    def own_to(phase, block, k):
+        send(phase, {2: 0, -2: 1}.get(k, 2), block.at[z], block.at[z], z_peer(k % n))
+
+    def gather_wrap():
+        @pl.when(z == 0)
+        def _():
+            pl.semaphore_wait(ready_sem.at[0], 1)
+            own_to(GATHER_S, xs, -2)
+            own_to(GATHER_R, xr, -2)
+
+        @pl.when(z < 2)
+        def _():
+            pl.semaphore_wait(ready_sem.at[1], 1)
+
+        @pl.when(z == 0)
+        def _():
+            own_to(GATHER_S, xs, -1)
+            own_to(GATHER_R, xr, -1)
+
+        @pl.when(z == 1)
+        def _():
+            own_to(GATHER_S, xs, -2)
+            own_to(GATHER_R, xr, -2)
 
     def relay(phase, block, sign):
         source = at(-2 * sign)
@@ -181,7 +216,17 @@
             bytes_of(block.at[pl.ds(0, 6)], send_sem.at[phase])
 
     columns.wait()
-    pl.semaphore_wait(barrier, len(peers))
+    pl.semaphore_wait(barrier, len(peers) + jnp.minimum(z, 2))
+
+    @pl.when(z == n - 2)
+    def _():
+        pl.semaphore_signal(ready_sem.at[0], inc=1, device_id=z_peer(2), device_id_type=MESH)
+
+    @pl.when(z == n - 1)
+    def _():
+        for k in (1, 2):
+            pl.semaphore_signal(ready_sem.at[1], inc=1, device_id=z_peer(k), device_id_type=MESH)
+
     gather_start(GATHER_S, xs, (2, -2, 1, -1))
     pairs = [
         pltpu.make_async_remote_copy(
@@ -242,6 +287,7 @@
     place_all = dot(holds.astype(BF16), before).astype(jnp.int32)
     combine = jnp.where((holds > 0.5) & (place_all == number % CAP), weight, 0.0).astype(BF16)
 
+    gather_wrap()
     in_turn(
         functools.partial(relay, GATHER_S, xs),
         functools.partial(relay, GATHER_R, xr),
@@ -305,9 +351,17 @@
         j = (x + m) % n
         columns = w2[:, :, pl.ds(pl.multiple_of(j * width, 128), width)]
         y[m] = dot(routed, columns.reshape(2 * units, width)).astype(BF16).reshape(n, CAP, width)
-        for k in [*far_first, 0] if m else far_first:
-            peer = {"expert": j, "group": at(k) * 2 + c}
-            send(RETURN_R, 0, y.at[m, at(k)], placed.at[here], peer)
+    for t in range(n):
+        for m in [*far_first, 0]:
+            peer = {"expert": (x + m) % n, "group": t * 2 + c}
+            if m:
+                send(RETURN_R, 0, y.at[m, t], placed.at[here], peer)
+            else:
+
+                @pl.when(z != t)
+                def _():
+                    send(RETURN_R, 0, y.at[0, t], placed.at[here], peer)
+
     placed[here] = y[0, z]
 
     loads[3].wait()
@@ -315,8 +369,12 @@
     arrived(SHARE, 0, hids.at[pl.ds(0, n - 1)])
     shared = dot(hids[...].reshape(total, 2 * units), s2[...].reshape(2 * units, width))
     ret_s[...] = shared.astype(BF16).reshape(n, rows, width)
-    for k in far_first:
-        send(RETURN_S, 0, ret_s.at[at(k)], got_s.at[z], z_peer(k))
+    for t in range(n):
+
+        @pl.when(z != t)
+        def _():
+            send(RETURN_S, 0, ret_s.at[t], got_s.at[z], {"group": t * 2 + c})
+
     got_s[z] = ret_s[z]
 
     arrived(RETURN_R, 0, placed.at[pl.ds(0, n * n - 1)])
@@ -386,6 +444,7 @@
                 pltpu.SemaphoreType.DMA((4,)),
                 pltpu.SemaphoreType.DMA((SENDS,)),
                 pltpu.SemaphoreType.DMA((SENDS, ARRIVALS)),
+                pltpu.SemaphoreType.REGULAR((2,)),
             ],
             compiler_params=pltpu.CompilerParams(
                 collective_id=0, has_side_effects=True, vmem_limit_bytes=48 << 20

time: 47.7 us -> 45.9 us (0.962)
  the two profiles are of different devices: /device:TPU:96 before, /device:TPU:48 now
where the time goes in v2:
time: 45.9 us; the launch traced here: 45.8 us
  Pallas kernels  45.2 us (98%)
  local copies, waits for them, and re-layouts  0.61 us (1%)
    pallas_call x1, Pallas kernels, layer(): pl.pallas_call(functools.partial(kernel, n), name='moe_layer', out_shape=...  45.2 us

profile of v2, /device:TPU:48, one launch (start us, length us, event | category | flops | bytes accessed | tf_op | source)
XLA Modules:
  0.0 45.8 jit_solution(13262606700396167257)
XLA Ops:
  0.0 45.2 %moe_layer.1 = bf16[16,896]{1,0:T(8,128)(2,1)S(1)} custom-call(bf16[16,7168]{1,0:T(8,128)(2,1)} %tok_hbm.1, s32[8,16]{1,0:T(8,128)} %bitcast.8, bf16[8,16]{1,0:T(8,128)(2,1)} %bitcast.9, bf16[14336,128]{1,0:T(8,128)(2,1)} %bitcast.5, bf16[128,7168]{1,0:T(8,128)(2,1)} %bitcast.6, bf16[1792,128]{1,0:T(8,128)(2,1)} %bitcast.7, bf16[128,896]{1,0:T(8,128)(2,1)} %s2_hbm.1), custom_call_target="tpu_custom_call" | custom-call | tf_op jit(solution)/shard_map/moe_layer/pallas_call | solution.py:413
  45.2 0.6 %copy.9 = bf16[16,896]{1,0:T(8,128)(2,1)} copy(bf16[16,896]{1,0:T(8,128)(2,1)S(1)} %moe_layer.1) | data formatting | bytes 57344

commit v3 on v2

--- a/solution.py
+++ b/solution.py
@@ -93,8 +93,17 @@
     )
     columns.start()
     barrier = pltpu.get_barrier_semaphore()
-    peers = [z_peer(n - 2), z_peer(n - 1), sibling]
-    peers += [x_peer(k) for k in range(1, n)]
+    peers = [z_peer(n - 2), z_peer(n - 1)]
+
+    def rank_of(place):
+        return jnp.where(place > n // 2, 2 * (n - place), jnp.maximum(2 * place - 1, 0))
+
+    rank = rank_of(x)
+
+
+    @pl.when(c == 0)
+    def _():
+        pl.semaphore_signal(barrier, inc=1, device_id=sibling, device_id_type=MESH)
 
     for k in (2, 1):
 
@@ -104,6 +113,12 @@
 
     for peer in peers:
         pl.semaphore_signal(barrier, inc=1, device_id=peer, device_id_type=MESH)
+    for k in range(1, n):
+
+        @pl.when(rank_of((x + k) % n) > rank)
+        def _():
+            pl.semaphore_signal(barrier, inc=1, device_id=x_peer(k), device_id_type=MESH)
+
 
     tokens = [
         pltpu.make_async_copy(
@@ -216,7 +231,12 @@
             bytes_of(block.at[pl.ds(0, 6)], send_sem.at[phase])
 
     columns.wait()
-    pl.semaphore_wait(barrier, len(peers) + jnp.minimum(z, 2))
+    pl.semaphore_wait(barrier, len(peers) + jnp.minimum(z, 2) + c + rank)
+
+    @pl.when(c == 1)
+    def _():
+        pl.semaphore_signal(ready_sem.at[2], inc=1, device_id=sibling, device_id_type=MESH)
+
 
     @pl.when(z == n - 2)
     def _():
@@ -241,7 +261,11 @@
             ((s1_hbm, s1), (w1_hbm, w1), (w2_hbm, w2), (s2_hbm, s2))
         )
     ]
-    pairs[0].start()
+
+    @pl.when(c == 1)
+    def _():
+        pairs[0].start()
+
 
     bytes_of(tok, local_sem.at[7])
     loads[0].wait()
@@ -256,8 +280,12 @@
     packed = dot(picker, tok[...].reshape(total, width)).astype(BF16)
     xr[z] = packed
     gather_start(GATHER_R, xr, (2, -2, 1, -1))
-    for copy in pairs[1:]:
-        copy.start()
+
+    @pl.when(c == 1)
+    def _():
+        for copy in pairs[1:]:
+            copy.start()
+
 
     def pair_arrived(i, target):
         pltpu.make_async_remote_copy(
@@ -274,6 +302,14 @@
     expand[...] = one_hot(lane % 256 == feature * 2 + lane // 256)
     to, source = iota((256, 256), 0), iota((256, 256), 1)
     apart[...] = one_hot(source == to % 128 * 2 + to // 128)
+
+    for k in range(1, n):
+
+        @pl.when(rank_of((x + k) % n) < rank)
+        def _():
+            pl.semaphore_signal(
+                ready_sem.at[3], inc=1, device_id=x_peer(k), device_id_type=MESH
+            )
 
     loads[1].wait()
     number = iota((CAP * n, rows), 0)
@@ -287,6 +323,12 @@
     place_all = dot(holds.astype(BF16), before).astype(jnp.int32)
     combine = jnp.where((holds > 0.5) & (place_all == number % CAP), weight, 0.0).astype(BF16)
 
+    @pl.when(c == 0)
+    def _():
+        pl.semaphore_wait(ready_sem.at[2], 1)
+        for copy in pairs:
+            copy.start()
+
     gather_wrap()
     in_turn(
         functools.partial(relay, GATHER_S, xs),
@@ -302,6 +344,10 @@
         s1d[q * 128 : q * 128 + 128, 2 * units : 4 * units] = split[128:]
 
     gather_end(GATHER_S, xs)
+    @pl.when(rank < n - 1)
+    def _():
+        pl.semaphore_wait(ready_sem.at[3], n - 1 - rank)
+
     mine = dot(xs[...].reshape(total, width), s1d[...]).astype(BF16)
     part[...] = mine.reshape(n, rows, 4 * units)
     for k in far_first:
@@ -444,7 +490,7 @@
                 pltpu.SemaphoreType.DMA((4,)),
                 pltpu.SemaphoreType.DMA((SENDS,)),
                 pltpu.SemaphoreType.DMA((SENDS, ARRIVALS)),
-                pltpu.SemaphoreType.REGULAR((2,)),
+                pltpu.SemaphoreType.REGULAR((4,)),
             ],
             compiler_params=pltpu.CompilerParams(
                 collective_id=0, has_side_effects=True, vmem_limit_bytes=48 << 20

time: 45.9 us -> 44.3 us (0.965)
  the two profiles are of different devices: /device:TPU:48 before, /device:TPU:96 now
where the time goes in v3:
time: 44.3 us; the launch traced here: 44.1 us
  Pallas kernels  43.5 us (98%)
  local copies, waits for them, and re-layouts  0.61 us (1%)
    pallas_call x1, Pallas kernels, layer(): pl.pallas_call(functools.partial(kernel, n), name='moe_layer', out_shape=...  43.5 us

profile of v3, /device:TPU:96, one launch (start us, length us, event | category | flops | bytes accessed | tf_op | source)
XLA Modules:
  0.0 44.1 jit_solution(18052062006512984574)
XLA Ops:
  0.0 43.5 %moe_layer.1 = bf16[16,896]{1,0:T(8,128)(2,1)S(1)} custom-call(bf16[16,7168]{1,0:T(8,128)(2,1)} %tok_hbm.1, s32[8,16]{1,0:T(8,128)} %bitcast.8, bf16[8,16]{1,0:T(8,128)(2,1)} %bitcast.9, bf16[14336,128]{1,0:T(8,128)(2,1)} %bitcast.5, bf16[128,7168]{1,0:T(8,128)(2,1)} %bitcast.6, bf16[1792,128]{1,0:T(8,128)(2,1)} %bitcast.7, bf16[128,896]{1,0:T(8,128)(2,1)} %s2_hbm.1), custom_call_target="tpu_custom_call" | custom-call | tf_op jit(solution)/shard_map/moe_layer/pallas_call | solution.py:459
  43.5 0.6 %copy.9 = bf16[16,896]{1,0:T(8,128)(2,1)} copy(bf16[16,896]{1,0:T(8,128)(2,1)S(1)} %moe_layer.1) | data formatting | bytes 57344

commit v4 on v3

--- a/solution.py
+++ b/solution.py
@@ -361,6 +361,20 @@
     )
     spread[...] = dot(stacked, expand[...]).astype(BF16).reshape(pieces, n, CAP * n, 512)
 
+    def share():
+        arrived(SPREAD, 0, parts.at[pl.ds(0, n - 1)])
+        pre = jnp.sum(parts[...].astype(F32), axis=0)
+        gate, up = pre[:, : 2 * units], pre[:, 2 * units :]
+        hidden = (gate / (1.0 + jnp.exp(-gate)) * up).astype(BF16)
+        hid[...] = hidden
+        for k in far_first:
+            send(SHARE, 0, hid, hids.at[x], x_peer(k))
+        hids[x] = hidden
+
+    @pl.when(c == 1)
+    def _():
+        share()
+
     loads[4].wait()
     pair_arrived(1, w1)
     left = jnp.concatenate(
@@ -381,14 +395,9 @@
     gate, up = both[: CAP * n], both[CAP * n :]
     routed = (gate / (1.0 + jnp.exp(-gate)) * up).astype(BF16)
 
-    arrived(SPREAD, 0, parts.at[pl.ds(0, n - 1)])
-    pre = jnp.sum(parts[...].astype(F32), axis=0)
-    gate, up = pre[:, : 2 * units], pre[:, 2 * units :]
-    hidden = (gate / (1.0 + jnp.exp(-gate)) * up).astype(BF16)
-    hid[...] = hidden
-    for k in far_first:
-        send(SHARE, 0, hid, hids.at[x], x_peer(k))
-    hids[x] = hidden
+    @pl.when(c == 0)
+    def _():
+        share()
 
     loads[5].wait()
     pair_arrived(2, w2)

time: 44.3 us -> 45.4 us (1.025)
  the two profiles are of different devices: /device:TPU:96 before, /device:TPU:1 now
where the time goes in v4:
time: 45.4 us; the launch traced here: 45.3 us
  Pallas kernels  44.6 us (98%)
  local copies, waits for them, and re-layouts  0.61 us (1%)
    pallas_call x1, Pallas kernels, layer(): pl.pallas_call(functools.partial(kernel, n), name='moe_layer', out_shape=...  44.6 us

profile of v4, /device:TPU:1, one launch (start us, length us, event | category | flops | bytes accessed | tf_op | source)
XLA Modules:
  0.0 45.3 jit_solution(6454246843085689008)
XLA Ops:
  0.0 44.6 %moe_layer.1 = bf16[16,896]{1,0:T(8,128)(2,1)S(1)} custom-call(bf16[16,7168]{1,0:T(8,128)(2,1)} %tok_hbm.1, s32[8,16]{1,0:T(8,128)} %bitcast.8, bf16[8,16]{1,0:T(8,128)(2,1)} %bitcast.9, bf16[14336,128]{1,0:T(8,128)(2,1)} %bitcast.5, bf16[128,7168]{1,0:T(8,128)(2,1)} %bitcast.6, bf16[1792,128]{1,0:T(8,128)(2,1)} %bitcast.7, bf16[128,896]{1,0:T(8,128)(2,1)} %s2_hbm.1), custom_call_target="tpu_custom_call" | custom-call | tf_op jit(solution)/shard_map/moe_layer/pallas_call | solution.py:468
  44.6 0.6 %copy.9 = bf16[16,896]{1,0:T(8,128)(2,1)} copy(bf16[16,896]{1,0:T(8,128)(2,1)S(1)} %moe_layer.1) | data formatting | bytes 57344
